TPU v7x, 32 devices: a whole 2x2x4 slice. The times are simulated.
32 devices in a mesh: tok: 8 (over z, y), voc: 4 (over x, core).
Axes of the slice: x: 2, y: 2, z: 4, core: 2. Of those that a mesh axis runs over, the one named last changes fastest.
Arguments:
- hidden: bfloat16 [1024, 2048], P('tok'), may hold values from -6 to 6
- mix_weight: bfloat16 [4, 2048], P(None, 'voc'), may hold values from -0.0546875 to 0.0546875
- comp_proj: bfloat16 [2048, 4, 2048], P(None, None, 'voc'), may hold values from -0.110485435 to 0.110485435
- vocab_weight: bfloat16 [2048, 1024], P(None, 'voc'), may hold values from -0.625 to 0.625
- log_normalizer: float32 [4, 1024], P(None, 'tok'), may hold values from 11 to 11.6
- targets: int32 [1024], P('tok'), may hold values from 0 to 1023
- loss_grad: float32 [1024], P('tok'), may hold values from 0.5 to 1.5
Outputs:
- hidden_grad: bfloat16 [1024, 2048], P('tok', 'voc')
- proj_grad: bfloat16 [2048, 4, 2048], P('tok', None, 'voc')
- vocab_grad: bfloat16 [2048, 1024], P('tok', 'voc')
All inputs are finite; a program needn't handle non-finite values.
Results may differ from a plain program's by a relative error of at most 0.02.
Values may be sent and summed in bfloat16 or wider, within the bound.
A program may use at most 64 MiB of HBM per device.

v0:
```python
import jax
import jax.numpy as jnp
from jax import lax
from jax.sharding import PartitionSpec as P


def body(hidden, mix_weight, comp_proj, vocab_weight, log_normalizer, targets, loss_grad):
    voc_place = lax.axis_index("voc")
    own_cols = comp_proj.shape[2]
    own_vocab = vocab_weight.shape[1]
    pre_act = jnp.einsum("td,dke->ekt", hidden, comp_proj, preferred_element_type=jnp.float32)
    context_own = jnp.tanh(pre_act).astype(jnp.bfloat16)
    own_hidden = lax.dynamic_slice_in_dim(hidden, voc_place * own_cols, own_cols, 1)
    mixing_part = jnp.einsum(
        "kd,td->kt", mix_weight, own_hidden, preferred_element_type=jnp.float32
    )
    mixing = lax.psum(mixing_part, "voc")
    context_full = lax.all_gather(context_own, "voc", axis=0, tiled=True)
    logits = jnp.einsum(
        "dkt,dv->ktv", context_full, vocab_weight, preferred_element_type=jnp.float32
    )
    vocab_ids = voc_place * own_vocab + lax.iota(jnp.int32, own_vocab)
    onehot = (targets[:, None] == vocab_ids[None, :]).astype(jnp.float32)
    target_part = jnp.sum(logits * onehot[None], axis=2)
    target = lax.psum(target_part, "voc")
    exp_mix = jnp.exp(mixing)
    weights = exp_mix / jnp.sum(exp_mix, axis=0, keepdims=True)
    likely = jnp.exp(target - log_normalizer)
    joint_mass = weights * likely
    posterior = joint_mass / jnp.sum(joint_mass, axis=0, keepdims=True)
    factor = loss_grad[None, :] * posterior
    logit_grad = (
        factor[:, :, None] * (jnp.exp(logits - log_normalizer[:, :, None]) - onehot[None])
    ).astype(jnp.bfloat16)
    mixing_grad = loss_grad[None, :] * (weights - posterior)
    rows_part = context_full
    vocab_grad = lax.psum_scatter(
        jnp.einsum("dkt,ktv->dv", rows_part, logit_grad, preferred_element_type=jnp.float32).astype(
            jnp.bfloat16
        ),
        "tok",
        scatter_dimension=0,
        tiled=True,
    )
    rows_part = vocab_weight
    context_grad = lax.psum_scatter(
        jnp.einsum("dv,ktv->dkt", rows_part, logit_grad, preferred_element_type=jnp.float32).astype(
            jnp.bfloat16
        ),
        "voc",
        scatter_dimension=0,
        tiled=True,
    ).astype(jnp.float32)
    own_f = context_own.astype(jnp.float32)
    pre_grad = (context_grad * (1.0 - own_f * own_f)).astype(jnp.bfloat16)
    rows_part = comp_proj
    hidden_sum = lax.psum_scatter(
        jnp.einsum("jke,ekt->jt", rows_part, pre_grad, preferred_element_type=jnp.float32).astype(
            jnp.bfloat16
        ),
        "voc",
        scatter_dimension=0,
        tiled=True,
    ).astype(jnp.float32)
    mix_term = jnp.einsum(
        "kt,kd->td", mixing_grad, mix_weight.astype(jnp.float32), precision=lax.Precision.HIGHEST
    )
    hidden_grad = (hidden_sum.T + mix_term).astype(jnp.bfloat16)
    hidden_rows = lax.all_to_all(hidden, "tok", split_axis=1, concat_axis=0, tiled=True)
    proj_sum = jnp.einsum(
        "tr,ekt->rke",
        hidden_rows,
        lax.all_gather(pre_grad, "tok", axis=2, tiled=True),
        preferred_element_type=jnp.float32,
    )
    proj_grad = proj_sum.astype(jnp.bfloat16)
    return (hidden_grad, proj_grad, vocab_grad)


def solution(mesh):
    in_specs = (
        P("tok", None),
        P(None, "voc"),
        P(None, None, "voc"),
        P(None, "voc"),
        P(None, "tok"),
        P("tok"),
        P("tok"),
    )
    out_specs = (P("tok", "voc"), P("tok", None, "voc"), P("tok", "voc"))
    return jax.shard_map(body, mesh=mesh, in_specs=in_specs, out_specs=out_specs, check_vma=False)
```

profile of v0, /device:TPU:0, one launch (start us, length us, event | category | flops | bytes accessed | tf_op | source)
XLA Modules:
  0.0 265.9 jit_solution(5083062717808202142)
XLA Ops:
  7.2 0.0 copy-start
  7.2 0.0 all-gather.3.cloned.1.call-start
  7.2 8.8 %fusion.22 = bf16[512,4,128]{2,0,1:T(8,128)(2,1)} fusion(bf16[2048,4,512]{2,1,0:T(4,128)(2,1)} %param.9, bf16[128,2048]{1,0:T(8,128)(2,1)} %param.7), kind=kOutput, calls=%fused_computation.15 | convolution fusion | flops 1074003968 | bytes 9437184 | tf_op jit(solution)/shard_map/td,dke->ekt/dot_general | solution.py:11
  16.0 0.0 all-gather.3.cloned.1.call-update
  16.1 0.0 reduce-scatter.4.cloned.1.call-start
  16.1 1.1 convolution_bitcast_fusion.1
  17.2 0.1 compare_convert_fusion
  17.3 0.0 copy-start.3
  17.3 24.2 %all-gather.3.cloned.1.call-done = bf16[2048,4,128]{2,0,1:T(8,128)(2,1)} async-done(((bf16[512,4,128]{2,0,1:T(8,128)(2,1)}), bf16[2048,4,128]{2,0,1:T(8,128)(2,1)}) %all-gather.3.cloned.1.call-update) | async-done | bytes 2097168 | tf_op jit(solution)/shard_map/all_gather | solution.py:18
  41.5 2.4 multiply_reduce_fusion
  43.9 5.9 %all-reduce = (f32[4,128]{1,0:T(4,128)S(1)}, f32[4,128]{1,0:T(4,128)S(1)}) all-reduce(f32[4,128]{1,0:T(4,128)S(1)} %get-tuple-element.10, f32[4,128]{1,0:T(4,128)S(1)} %convolution_bitcast_fusion.1), channel_id=1, replica_groups=mesh['tok'=8,'voc'=4] {'voc'}, use_global_device_ids=true, to_apply=%region_3.0 | all-reduce | flops 1024 | bytes 8192 | tf_op jit(solution)/shard_map/psum | solution.py:25
  49.9 2.2 fusion.4
  52.1 0.0 reduce-scatter.4.cloned.1.call-update
  52.1 0.0 reduce-scatter.6.cloned.1.call-start
  52.2 32.3 %reduce-scatter.4.cloned.1.call-done = bf16[512,4,128]{2,0,1:T(8,128)(2,1)} async-done(((bf16[2048,4,128]{2,0,1:T(8,128)(2,1)}), bf16[512,4,128]{2,0,1:T(8,128)(2,1)}) %reduce-scatter.4.cloned.1.call-update) | async-done | bytes 524304 | tf_op jit(solution)/shard_map/reduce_scatter | solution.py:46
  84.5 2.0 multiply_convert_fusion
  86.6 7.6 %fusion.12 = bf16[2048,128]{0,1:T(8,128)(2,1)} fusion(bf16[512,4,128]{2,0,1:T(8,128)(2,1)} %multiply_convert_fusion, bf16[2048,4,512]{2,1,0:T(4,128)(2,1)} %param.9), kind=kOutput, calls=%fused_computation.10 | convolution fusion | flops 1074003968 | bytes 9437184 | tf_op jit(solution)/shard_map/jke,ekt->jt/dot_general | solution.py:58
  94.2 0.0 reduce-scatter.6.cloned.1.call-update
  94.2 0.0 all-gather.5.cloned.1.call-start
  94.2 0.5 all-gather.5.cloned.1.call-update
  94.8 0.0 reduce-scatter.8.cloned.1.call-start
  94.8 2.9 %fusion.5 = bf16[2048,256]{1,0:T(8,128)(2,1)} fusion(bf16[2048,4,128]{2,0,1:T(8,128)(2,1)S(1)} %copy-done.1, f32[4,128,256]{2,1,0:T(8,128)} %copy-done.2, f32[4,128]{1,0:T(4,128)S(1)} %copy-done.4, f32[4,128]{1,0:T(4,128)S(1)} %broadcast_multiply_fusion, f32[128,256]{1,0:T(8,128)S(1)} %compare_convert_fusion), kind=kOutput, calls=%fused_computation.7 | convolution fusion | flops 537919488 | bytes 3805184 | tf_op jit(solution)/shard_map/dkt,ktv->dv/dot_general | solution.py:38
  97.7 0.0 reduce-scatter.8.cloned.1.call-update
  97.7 1.9 copy.38
  99.6 5.5 %all-to-all-start = ((bf16[128,8,256]{2,0,1:T(8,128)(2,1)}), bf16[128,8,256]{2,0,1:T(8,128)(2,1)S(1)}, u32[]{:S(2)}, u32[]{:S(2)}) async-start(bf16[128,8,256]{2,0,1:T(8,128)(2,1)} %bitcast.47), calls=%async_computation.2 | async-start | bytes 1048576 | tf_op jit(solution)/shard_map/all_to_all | solution.py:69
  105.1 10.9 %reduce-scatter.6.cloned.1.call-done = bf16[512,128]{0,1:T(8,128)(2,1)} async-done(((bf16[2048,128]{0,1:T(8,128)(2,1)}), bf16[512,128]{0,1:T(8,128)(2,1)}) %reduce-scatter.6.cloned.1.call-update) | async-done | bytes 131088 | tf_op jit(solution)/shard_map/reduce_scatter | solution.py:57
  116.0 1.9 fusion.25
  117.9 1.6 all-to-all-done
  119.5 73.7 %all-gather.5.cloned.1.call-done = bf16[512,4,1024]{2,0,1:T(8,128)(2,1)} async-done(((bf16[512,4,128]{2,0,1:T(8,128)(2,1)}), bf16[512,4,1024]{2,0,1:T(8,128)(2,1)}) %all-gather.5.cloned.1.call-update) | async-done | bytes 4194320 | tf_op jit(solution)/shard_map/all_gather | solution.py:73
  193.2 3.4 %fusion.15 = bf16[256,4,512]{0,2,1:T(8,128)(2,1)S(1)} fusion(bf16[512,4,1024]{2,0,1:T(8,128)(2,1)} %all-gather.5.cloned.1.call-done, bf16[1024,256,1]{1,0,2:T(8,128)(2,1)S(1)} %bitcast.49), kind=kOutput, calls=%fused_computation.12 | convolution fusion | flops 1074266112 | bytes 5767168 | tf_op jit(solution)/shard_map/tr,ekt->rke/dot_general | solution.py:70
  196.6 1.8 copy.16
  198.4 61.0 %reduce-scatter.8.cloned.1.call-done = bf16[256,256]{1,0:T(8,128)(2,1)} async-done(((bf16[2048,256]{1,0:T(8,128)(2,1)}), bf16[256,256]{1,0:T(8,128)(2,1)}) %reduce-scatter.8.cloned.1.call-update) | async-done | bytes 131088 | tf_op jit(solution)/shard_map/reduce_scatter | solution.py:37
  (18 shorter events, 0.1 us)
Async XLA Ops:
  7.2 34.3 %copy-start = (bf16[2048,256]{1,0:T(8,128)(2,1)S(1)}, bf16[2048,256]{1,0:T(8,128)(2,1)}, u32[]{:S(2)}) copy-start(bf16[2048,256]{1,0:T(8,128)(2,1)} %param.10) | copy-start | bytes 3145732
  7.2 8.9 %copy-start.5 = (bf16[4,512]{1,0:T(4,128)(2,1)S(1)}, bf16[4,512]{1,0:T(4,128)(2,1)}, u32[]{:S(2)}) copy-start(bf16[4,512]{1,0:T(4,128)(2,1)} %param.8) | copy-start | bytes 12292
  7.2 10.0 %copy-start.7 = (s32[128]{0:T(128)S(1)}, s32[128]{0:T(128)}, u32[]{:S(2)}) copy-start(s32[128]{0:T(128)} %param.12) | copy-start | bytes 1540
  7.2 34.3 %all-gather.3.cloned.1.call-start = ((), (), s32[]{:S(2)}) async-start(), calls=%async_computation.4 | async-start | bytes 2621440 | tf_op jit(solution)/shard_map/all_gather | solution.py:18
  16.0 33.8 %copy-start.4 = (f32[4,128]{1,0:T(4,128)S(1)}, f32[4,128]{1,0:T(4,128)}, u32[]{:S(2)}) copy-start(f32[4,128]{1,0:T(4,128)} %param.11) | copy-start | bytes 6148
  16.0 33.8 %copy-start.6 = (f32[128]{0:T(128)S(1)}, f32[128]{0:T(128)}, u32[]{:S(2)}) copy-start(f32[128]{0:T(128)} %param.13) | copy-start | bytes 1540
  16.1 68.5 %reduce-scatter.4.cloned.1.call-start = ((), (), s32[]{:S(2)}) async-start(), calls=%async_computation.5 | async-start | bytes 2621440 | tf_op jit(solution)/shard_map/reduce_scatter | solution.py:46
  17.3 67.3 %copy-start.3 = (bf16[512,4,128]{2,0,1:T(8,128)(2,1)S(1)}, bf16[512,4,128]{2,0,1:T(8,128)(2,1)}, u32[]{:S(2)}) copy-start(bf16[512,4,128]{2,0,1:T(8,128)(2,1)} %fusion.22) | copy-start | bytes 1572868
  43.9 42.7 %copy-start.2 = (f32[4,128,256]{2,1,0:T(8,128)}, f32[4,128,256]{2,1,0:T(8,128)S(1)}, u32[]{:S(2)}) copy-start(f32[4,128,256]{2,1,0:T(8,128)S(1)} %get-tuple-element.11) | copy-start | bytes 1572868
  52.1 63.9 %reduce-scatter.6.cloned.1.call-start = ((), (), s32[]{:S(2)}) async-start(), calls=%async_computation.6 | async-start | bytes 655360 | tf_op jit(solution)/shard_map/reduce_scatter | solution.py:57
  86.6 8.2 %copy-start.1 = (bf16[2048,4,128]{2,0,1:T(8,128)(2,1)S(1)}, bf16[2048,4,128]{2,0,1:T(8,128)(2,1)}, u32[]{:S(2)}) copy-start(bf16[2048,4,128]{2,0,1:T(8,128)(2,1)} %all-gather.3.cloned.1.call-done) | copy-start | bytes 6291460
  94.2 99.0 %all-gather.5.cloned.1.call-start = ((), (), s32[]{:S(2)}) async-start(), calls=%async_computation.7 | async-start | bytes 4718592 | tf_op jit(solution)/shard_map/all_gather | solution.py:73
  94.8 164.6 %reduce-scatter.8.cloned.1.call-start = ((), (), s32[]{:S(2)}) async-start(), calls=%async_computation.8 | async-start | bytes 1179648 | tf_op jit(solution)/shard_map/reduce_scatter | solution.py:37
  99.6 19.8 %all-to-all-start = ((bf16[128,8,256]{2,0,1:T(8,128)(2,1)}), bf16[128,8,256]{2,0,1:T(8,128)(2,1)S(1)}, u32[]{:S(2)}, u32[]{:S(2)}) async-start(bf16[128,8,256]{2,0,1:T(8,128)(2,1)} %bitcast.47), calls=%async_computation.2 | async-start | bytes 1048576 | tf_op jit(solution)/shard_map/all_to_all | solution.py:69
Sparse Core Ops, SparseCore 0:
  16.2 25.2 all-gather.2
  52.3 32.2 reduce-scatter.3
  94.3 21.6 reduce-scatter.5
  118.5 74.6 all-gather.4
  197.0 62.3 reduce-scatter.7
where the time goes:
time: 266 us
  waiting for transfers between devices  204 us (77%)
  matrix products  30.3 us (11%)
  between operations  13.9 us (5%)
  blocking collectives  5.89 us (2%)
  starting transfers between devices  5.71 us (2%)
  local copies, waits for them, and re-layouts  3.73 us (1%)
    all_gather x1, waiting for transfers between devices, body(): lax.all_gather(pre_grad, 'tok', axis=2, tiled=True)  73.7 us
    reduce_scatter x1, waiting for transfers between devices, body(): lax.psum_scatter(jnp.einsum('dkt,ktv->dv', rows_part, logit_grad, preferr...  61 us
    reduce_scatter x1, waiting for transfers between devices, body(): lax.psum_scatter(jnp.einsum('dv,ktv->dkt', rows_part, logit_grad, preferr...  32.3 us
    all_gather x1, waiting for transfers between devices, body(): context_full = lax.all_gather(context_own, 'voc', axis=0, tiled=True)  24.2 us
    reduce_scatter x1, waiting for transfers between devices, body(): lax.psum_scatter(jnp.einsum('jke,ekt->jt', rows_part, pre_grad, preferred...  10.9 us
    dot_general x1, matrix products, body(): jnp.einsum('td,dke->ekt', hidden, comp_proj, preferred_element_type=jnp.f...  8.78 us
    dot_general x1, matrix products, body(): jnp.einsum('jke,ekt->jt', rows_part, pre_grad, preferred_element_type=jnp...  7.59 us
    psum x1, blocking collectives, body(): target = lax.psum(target_part, 'voc')  5.89 us
  transfers between devices with their start and end apart: 6, of which 6 were waited for; matrix products, arithmetic and copies ran while one was open for 5% of the time, Pallas kernels for 0%

commit v1 on v0

v1 whole, which is shorter than its diff:
```python
import functools

import jax
import jax.numpy as jnp
from jax import lax
from jax.experimental import pallas as pl
from jax.experimental.pallas import tpu as pltpu
from jax.sharding import PartitionSpec as P

MESH = pl.DeviceIdType.MESH
F32 = jnp.float32
BF16 = jnp.bfloat16
NT = (((1,), (1,)), ((), ()))
TN = (((0,), (0,)), ((), ()))


def column(row, lanes):
    wide = jnp.broadcast_to(row, (128, row.shape[1])).T
    return jnp.concatenate([wide] * (lanes // 128), axis=1)


def kernel(
    M, N,
    hidden, mix, proj_hbm, vw, logz, targets, loss,
    out_hidden, out_proj, out_vocab,
    w, ctx, mix_all, hblk, hrow, logit, lg, tgt,
    cgs, cgr, cgx, xr, own_cg, vgb, vgr, pg, hss, hsr, own_hs, acc, mgrad,
    w_sem, ctx_s, ctx_f, ctx_r, mix_s, mix_r, hid_s, hid_r, tgt_s, tgt_r,
    cgp_s, cgp_r, cgx_s, cgx_r, vg_s, vg_r, hs_s, hs_r, ag_s, ag_r,
):
    K, D, E = w.shape
    T = hidden.shape[0]
    V = vw.shape[1]
    R = D // M
    half = N // 2
    Z = M // 2
    me_t = lax.axis_index("tok")
    me_v = lax.axis_index("voc")
    chip = me_v // 2
    core = me_v % 2
    partner = me_v + 1 - 2 * core
    z = me_t // 2
    y = me_t % 2
    ypart = me_t + 1 - 2 * y
    sends = []

    def remote(src, dst, ss, rs, dev):
        return pltpu.make_async_remote_copy(
            src_ref=src, dst_ref=dst, send_sem=ss, recv_sem=rs,
            device_id=dev, device_id_type=MESH,
        )

    def send(src, dst, ss, rs, dev):
        c = remote(src, dst, ss, rs, dev)
        c.start()
        sends.append((None, c))

    def arrived(ref, rs, ss):
        remote(ref, ref, ss, rs, {"voc": partner}).wait_recv()

    for k in range(K):
        pltpu.make_async_copy(proj_hbm.at[k], w.at[k], w_sem.at[k]).start()
    for j in range(M):
        hblk[j] = hidden[:, j * R:(j + 1) * R]

    bar = pltpu.get_barrier_semaphore()
    for d in range(1, M):
        pl.semaphore_signal(bar, inc=1, device_id={"tok": lax.rem(me_t + d, M)}, device_id_type=MESH)
    for d in range(1, N):
        pl.semaphore_signal(bar, inc=1, device_id={"voc": lax.rem(me_v + d, N)}, device_id_type=MESH)
    pl.semaphore_wait(bar, M + N - 2)

    for d in range(1, N):
        send(mix, mix_all.at[d], mix_s.at[d], mix_r.at[d], {"voc": lax.rem(me_v + d, N)})
    mix_all[0] = mix[...]
    for d in range(1, M):
        j = lax.rem(me_t + d, M)
        send(hblk.at[j], hrow.at[pl.ds(me_t * T, T)], hid_s.at[d], hid_r.at[d], {"tok": j})
    hrow[pl.ds(pl.multiple_of(me_t * T, T), T), :] = hblk[me_t]

    for k in range(K):
        pltpu.make_async_copy(proj_hbm.at[k], w.at[k], w_sem.at[k]).wait()
        ctx[me_v, k * T:(k + 1) * T, :] = jnp.tanh(
            jnp.dot(hidden[...], w[k], preferred_element_type=F32)
        ).astype(BF16)
        piece = ctx.at[me_v, pl.ds(k * T, T)]
        for i in range(1, half):
            send(piece, piece, ctx_s.at[i, k], ctx_r.at[me_v, k],
                 {"voc": lax.rem(chip + i, half) * 2 + core})
        send(piece, piece, ctx_s.at[0, k], ctx_r.at[me_v, k], {"voc": partner})

    def add_logits(s, first=False):
        part = jnp.dot(ctx[s], vw[pl.ds(pl.multiple_of(s * E, E), E), :],
                       preferred_element_type=F32)
        logit[...] = part if first else logit[...] + part

    add_logits(me_v, True)
    for k in range(K):
        arrived(ctx.at[partner, pl.ds(k * T, T)], ctx_r.at[partner, k], ctx_s.at[0, k])
    add_logits(partner)

    tcol = column(targets[...].astype(F32), V)
    ids = (me_v * V + lax.broadcasted_iota(jnp.int32, (T, V), 1)).astype(F32)
    onehot = (tcol == ids).astype(F32)
    for d in range(1, N):
        arrived(mix_all.at[d], mix_r.at[d], mix_s.at[d])
    mixing = jnp.zeros((K, T), F32)
    for d in range(N):
        s = lax.rem(me_v - d + N, N)
        mixing = mixing + lax.dot_general(
            mix_all[d], hidden[:, pl.ds(pl.multiple_of(s * E, E), E)], NT,
            preferred_element_type=F32)
    exp_mix = jnp.exp(mixing)
    weights = exp_mix / jnp.sum(exp_mix, axis=0, keepdims=True)

    for i in range(1, half):
        s = lax.rem(chip - i + half, half) * 2 + core
        for k in range(K):
            piece = ctx.at[s, pl.ds(k * T, T)]
            arrived(piece, ctx_r.at[s, k], ctx_s.at[i, k])
            send(piece, piece, ctx_f.at[i, k], ctx_r.at[s, k], {"voc": partner})
        add_logits(s)
    for i in range(1, half):
        s = lax.rem(chip - i + half, half) * 2 + 1 - core
        for k in range(K):
            arrived(ctx.at[s, pl.ds(k * T, T)], ctx_r.at[s, k], ctx_s.at[i, k])
        add_logits(s)

    lane = lax.broadcasted_iota(jnp.int32, (T, 128), 1)
    table = jnp.zeros((T, 128), F32)
    for k in range(K):
        part = jnp.sum(logit[k * T:(k + 1) * T, :] * onehot, axis=1, keepdims=True)
        table = jnp.where(lane == k, part, table)
    tgt[0] = table.T[0:8, :]
    for d in range(1, N):
        send(tgt.at[0], tgt.at[d], tgt_s.at[d], tgt_r.at[d], {"voc": lax.rem(me_v + d, N)})
    for k in range(K):
        rows = slice(k * T, (k + 1) * T)
        logit[rows, :] = jnp.exp(logit[rows, :] - column(logz[k:k + 1, :], V)) - onehot
    for d in range(1, N):
        arrived(tgt.at[d], tgt_r.at[d], tgt_s.at[d])
    target = tgt[0]
    for d in range(1, N):
        target = target + tgt[d]
    likely = jnp.exp(target[0:K, :] - logz[...])
    joint = weights * likely
    posterior = joint / jnp.sum(joint, axis=0, keepdims=True)
    factor = loss[...] * posterior
    mgrad[...] = loss[...] * (weights - posterior)
    for k in range(K):
        rows = slice(k * T, (k + 1) * T)
        lg[rows, :] = (column(factor[k:k + 1, :], V) * logit[rows, :]).astype(BF16)

    def cg_part(s, k):
        return lax.dot_general(
            lg[k * T:(k + 1) * T, :], vw[pl.ds(pl.multiple_of(s * E, E), E), :], NT,
            preferred_element_type=F32)

    for i in list(range(1, half)) + [0]:
        s = lax.rem(chip + i, half) * 2
        for k in range(K):
            cgs[i, k] = cg_part(s + 1 - core, k).astype(BF16)
            send(cgs.at[i, k], cgr.at[i, k], cgp_s.at[i, k], cgp_r.at[i, k], {"voc": partner})
        for k in range(K):
            part = cg_part(s + core, k)
            if i == 0:
                own_cg[k] = part
            else:
                arrived(cgr.at[i, k], cgp_r.at[i, k], cgp_s.at[i, k])
                cgx[i, k] = (part + cgr[i, k].astype(F32)).astype(BF16)
                send(cgx.at[i, k], xr.at[i, k], cgx_s.at[i, k], cgx_r.at[i, k], {"voc": s + core})

    for s in range(N):
        vgb[s * E:(s + 1) * E, :] = lax.dot_general(
            ctx[s], lg[...], TN, preferred_element_type=F32).astype(BF16)
    for d in range(1, M):
        j = lax.rem(me_t + d, M)
        send(vgb.at[pl.ds(j * R, R)], vgr.at[d], vg_s.at[d], vg_r.at[d], {"tok": j})

    def rows_of(t):
        return pl.ds(pl.multiple_of(t * T, T), T)

    def relay(t, k, way, dev, pred=None):
        piece = pg.at[k, rows_of(t)]
        c = remote(piece, piece, ag_s.at[way, t, k], ag_r.at[t, k], {"tok": dev})
        if pred is None:
            c.start()
        else:
            pl.when(pred)(c.start)
        sends.append((pred, c))

    has_r = z + 1 < Z
    has_l = z >= 1
    for k in range(K):
        total = own_cg[k]
        arrived(cgr.at[0, k], cgp_r.at[0, k], cgp_s.at[0, k])
        total = total + cgr[0, k].astype(F32)
        for i in range(1, half):
            arrived(xr.at[i, k], cgx_r.at[i, k], cgx_s.at[i, k])
            total = total + xr[i, k].astype(F32)
        c = ctx[me_v, k * T:(k + 1) * T, :].astype(F32)
        pg[k, rows_of(me_t), :] = (total * (1.0 - c * c)).astype(BF16)
        if Z > 1:
            relay(me_t, k, 0, me_t + 2, has_r)
            relay(me_t, k, 1, me_t - 2, has_l)
        relay(me_t, k, 2, ypart)

    def hid_part(s):
        total = jnp.zeros((T, E), F32)
        for k in range(K):
            total = total + lax.dot_general(
                pg[k, rows_of(me_t), :], w[k, pl.ds(pl.multiple_of(s * E, E), E), :], NT,
                preferred_element_type=F32)
        return total

    for d in range(1, N):
        s = lax.rem(me_v + d, N)
        hss[d] = hid_part(s).astype(BF16)
        send(hss.at[d], hsr.at[d], hs_s.at[d], hs_r.at[d], {"voc": s})
    own_hs[...] = hid_part(me_v)

    for d in range(1, M):
        src = lax.rem(me_t - d + M, M)
        arrived(hrow.at[pl.ds(src * T, T)], hid_r.at[d], hid_s.at[d])

    def pair(zz, first=False):
        t = zz * 2 + 1 - y
        both = pl.ds(pl.multiple_of(zz * 2 * T, 2 * T), 2 * T)
        left = hrow[both, :].T
        for k in range(K):
            arrived(pg.at[k, rows_of(t)], ag_r.at[t, k], ag_s.at[2, t, k])
            part = jnp.dot(left, pg[k, both, :], preferred_element_type=F32)
            acc[k] = part if first else acc[k] + part

    def pairs(d):
        if d == 0:
            pair(z, True)
        else:
            pl.when(z >= d)(lambda: pair(z - d))
            pl.when(z + d < Z)(lambda: pair(z + d))

    for d in range(1, Z):
        from_l = z >= d
        from_r = z + d < Z
        for k in range(K):
            for there, t, way, dev, more in (
                (from_l, me_t - 2 * d, 0, me_t + 2, has_r),
                (from_r, me_t + 2 * d, 1, me_t - 2, has_l),
            ):
                def _(t=t, k=k):
                    arrived(pg.at[k, rows_of(t)], ag_r.at[t, k], ag_s.at[2, t, k])
                pl.when(there)(_)
                if d < Z - 1:
                    relay(t, k, way, dev, there & more)
                relay(t, k, 2, ypart, there)
        pairs(d - 1)

    vtot = vgb[rows_r(me_t, R), :].astype(F32)
    for d in range(1, M):
        arrived(vgr.at[d], vg_r.at[d], vg_s.at[d])
        vtot = vtot + vgr[d].astype(F32)
    out_vocab[...] = vtot.astype(BF16)
    htot = own_hs[...]
    for d in range(1, N):
        arrived(hsr.at[d], hs_r.at[d], hs_s.at[d])
        htot = htot + hsr[d].astype(F32)
    mixf = mix[...].astype(F32)
    for k in range(K):
        htot = htot + column(mgrad[k:k + 1, :], E) * mixf[k:k + 1, :]
    out_hidden[...] = htot.astype(BF16)

    pairs(Z - 1)
    for k in range(K):
        out_proj[k] = acc[k].astype(BF16)
    for pred, c in sends:
        if pred is None:
            c.wait_send()
        else:
            pl.when(pred)(c.wait_send)


def rows_r(t, R):
    return pl.ds(pl.multiple_of(t * R, R), R)


def body(M, N, hidden, mix_weight, comp_proj, vocab_weight, log_normalizer, targets, loss_grad):
    T, D = hidden.shape
    K, E = mix_weight.shape
    V = vocab_weight.shape[1]
    R = D // M
    half = N // 2
    w = jnp.transpose(comp_proj, (1, 0, 2))
    vm = pltpu.VMEM
    dma = pltpu.SemaphoreType.DMA
    scratch = [
        vm((K, D, E), BF16), vm((N, K * T, E), BF16), vm((N, K, E), BF16),
        vm((M, T, R), BF16), vm((M * T, R), BF16), vm((K * T, V), F32), vm((K * T, V), BF16),
        vm((N, 8, T), F32),
        vm((half, K, T, E), BF16), vm((half, K, T, E), BF16),
        vm((half, K, T, E), BF16), vm((half, K, T, E), BF16),
        vm((K, T, E), F32), vm((D, V), BF16), vm((M, R, V), BF16),
        vm((K, M * T, E), BF16), vm((N, T, E), BF16), vm((N, T, E), BF16),
        vm((T, E), F32), vm((K, R, E), F32), vm((K, T), F32),
        dma((K,)), dma((half, K)), dma((half, K)), dma((N, K)), dma((N,)), dma((N,)),
        dma((M,)), dma((M,)), dma((N,)), dma((N,)),
        dma((half, K)), dma((half, K)), dma((half, K)), dma((half, K)),
        dma((M,)), dma((M,)), dma((N,)), dma((N,)), dma((3, M, K)), dma((M, K)),
    ]
    spec = pl.BlockSpec(memory_space=pltpu.VMEM)
    hidden_grad, proj_grad, vocab_grad = pl.pallas_call(
        functools.partial(kernel, M, N),
        out_shape=(
            jax.ShapeDtypeStruct((T, E), BF16),
            jax.ShapeDtypeStruct((K, R, E), BF16),
            jax.ShapeDtypeStruct((R, V), BF16),
        ),
        in_specs=[spec, spec, pl.BlockSpec(memory_space=pl.ANY), spec, spec, spec, spec],
        out_specs=(spec, spec, spec),
        scratch_shapes=scratch,
        compiler_params=pltpu.CompilerParams(
            collective_id=0, has_side_effects=True, vmem_limit_bytes=56 * 1024 * 1024
        ),
    )(hidden, mix_weight, w, vocab_weight, log_normalizer, targets[None, :], loss_grad[None, :])
    return hidden_grad, jnp.transpose(proj_grad, (1, 0, 2)), vocab_grad


def solution(mesh):
    in_specs = (
        P("tok", None),
        P(None, "voc"),
        P(None, None, "voc"),
        P(None, "voc"),
        P(None, "tok"),
        P("tok"),
        P("tok"),
    )
    out_specs = (P("tok", "voc"), P("tok", None, "voc"), P("tok", "voc"))
    return jax.shard_map(
        functools.partial(body, mesh.shape["tok"], mesh.shape["voc"]),
        mesh=mesh, in_specs=in_specs, out_specs=out_specs, check_vma=False,
    )
```

time: 266 us -> 108 us (0.41)
  the two profiles are of different devices: /device:TPU:0 before, /device:TPU:16 now
where the time goes in v1:
time: 108 us
  Pallas kernels  92.7 us (86%)
  local copies, waits for them, and re-layouts  14.4 us (13%)
    pallas_call x1, Pallas kernels, body(): pl.pallas_call(functools.partial(kernel, M, N), out_shape=(jax.ShapeDtype...  92.7 us
    unnamed x4, local copies, waits for them, and re-layouts  14.4 us

profile of v1, /device:TPU:16, one launch (start us, length us, event | category | flops | bytes accessed | tf_op | source)
XLA Modules:
  0.0 107.8 jit_solution(17591478922994630540)
XLA Ops:
  0.6 8.3 %copy.13 = bf16[2048,4,512]{2,0,1:T(8,128)(2,1)} copy(bf16[2048,4,512]{2,1,0:T(4,128)(2,1)} %param.9) | data formatting | bytes 16777216 | tf_op args[2]
  8.9 92.7 %shard_map.94 = (bf16[128,512]{1,0:T(8,128)(2,1)}, bf16[4,256,512]{2,1,0:T(8,128)(2,1)}, bf16[256,256]{1,0:T(8,128)(2,1)}) custom-call(bf16[128,2048]{1,0:T(8,128)(2,1)} %hidden.1, bf16[4,512]{1,0:T(4,128)(2,1)} %mix.1, bf16[4,2048,512]{2,1,0:T(8,128)(2,1)} %bitcast.6, bf16[2048,256]{1,0:T(8,128)(2,1)} %vw.1, f32[4,128]{1,0:T(4,128)} %logz.1, ...), custom_call_target="tpu_custom_call" | custom-call | tf_op jit(solution)/shard_map/pallas_call | solution.py:310
  101.6 3.0 %copy.11 = bf16[256,4,512]{2,1,0:T(4,128)(2,1)} copy(bf16[256,4,512]{2,0,1:T(8,128)(2,1)} %bitcast.7) | data formatting | bytes 2097152
  104.6 1.6 %copy.16 = bf16[128,512]{1,0:T(8,128)(2,1)} copy(bf16[128,512]{1,0:T(8,128)(2,1)} %get-tuple-element.15) | data formatting | bytes 262144
  106.2 1.6 %copy.17 = bf16[256,256]{1,0:T(8,128)(2,1)} copy(bf16[256,256]{1,0:T(8,128)(2,1)} %get-tuple-element.17) | data formatting | bytes 262144

commit v2 on v1

--- a/solution.py
+++ b/solution.py
@@ -23,10 +23,10 @@
     M, N,
     hidden, mix, proj_hbm, vw, logz, targets, loss,
     out_hidden, out_proj, out_vocab,
-    w, ctx, mix_all, hblk, hrow, logit, lg, tgt,
-    cgs, cgr, cgx, xr, own_cg, vgb, vgr, pg, hss, hsr, own_hs, acc, mgrad,
+    w, ctx, mix_all, hblk, hrow, htr, logit, lg, tgt,
+    cgs, cgr, cgx, xr, own_cg, vgb, vgy, vsum, vout, vin, pg, hss, hsr, own_hs, acc, psend, precv, mgrad,
     w_sem, ctx_s, ctx_f, ctx_r, mix_s, mix_r, hid_s, hid_r, tgt_s, tgt_r,
-    cgp_s, cgp_r, cgx_s, cgx_r, vg_s, vg_r, hs_s, hs_r, ag_s, ag_r,
+    cgp_s, cgp_r, cgx_s, cgx_r, vy_s, vy_r, vz_s, vz_r, hs_s, hs_r, ag_s, ag_r, pp_s, pp_r,
 ):
     K, D, E = w.shape
     T = hidden.shape[0]
@@ -61,7 +61,7 @@
     for k in range(K):
         pltpu.make_async_copy(proj_hbm.at[k], w.at[k], w_sem.at[k]).start()
     for j in range(M):
-        hblk[j] = hidden[:, j * R:(j + 1) * R]
+        hblk[j // 2, j % 2] = hidden[:, j * R:(j + 1) * R]
 
     bar = pltpu.get_barrier_semaphore()
     for d in range(1, M):
@@ -73,10 +73,11 @@
     for d in range(1, N):
         send(mix, mix_all.at[d], mix_s.at[d], mix_r.at[d], {"voc": lax.rem(me_v + d, N)})
     mix_all[0] = mix[...]
-    for d in range(1, M):
-        j = lax.rem(me_t + d, M)
-        send(hblk.at[j], hrow.at[pl.ds(me_t * T, T)], hid_s.at[d], hid_r.at[d], {"tok": j})
-    hrow[pl.ds(pl.multiple_of(me_t * T, T), T), :] = hblk[me_t]
+    for d in range(1, Z):
+        zz = lax.rem(z + d, Z)
+        send(hblk.at[zz], hrow.at[:, pl.ds(z * T, T)], hid_s.at[d], hid_r.at[d],
+             {"tok": zz * 2 + y})
+    hrow[:, rows_of(z, T), :] = hblk[z]
 
     for k in range(K):
         pltpu.make_async_copy(proj_hbm.at[k], w.at[k], w_sem.at[k]).wait()
@@ -173,20 +174,15 @@
     for s in range(N):
         vgb[s * E:(s + 1) * E, :] = lax.dot_general(
             ctx[s], lg[...], TN, preferred_element_type=F32).astype(BF16)
-    for d in range(1, M):
-        j = lax.rem(me_t + d, M)
-        send(vgb.at[pl.ds(j * R, R)], vgr.at[d], vg_s.at[d], vg_r.at[d], {"tok": j})
-
-    def rows_of(t):
-        return pl.ds(pl.multiple_of(t * T, T), T)
-
-    def relay(t, k, way, dev, pred=None):
-        piece = pg.at[k, rows_of(t)]
-        c = remote(piece, piece, ag_s.at[way, t, k], ag_r.at[t, k], {"tok": dev})
-        if pred is None:
-            c.start()
-        else:
-            pl.when(pred)(c.start)
+    for zz in range(Z):
+        send(vgb.at[pl.ds((zz * 2 + 1 - y) * R, R)], vgy.at[zz], vy_s.at[zz], vy_r.at[zz],
+             {"tok": ypart})
+
+    def relay(t, k, way, pred):
+        piece = pg.at[k, rows_of(t, T)]
+        c = remote(piece, piece, ag_s.at[way, t, k], ag_r.at[t, k],
+                   {"tok": me_t + 2 - 4 * way})
+        pl.when(pred)(c.start)
         sends.append((pred, c))
 
     has_r = z + 1 < Z
@@ -199,17 +195,16 @@
             arrived(xr.at[i, k], cgx_r.at[i, k], cgx_s.at[i, k])
             total = total + xr[i, k].astype(F32)
         c = ctx[me_v, k * T:(k + 1) * T, :].astype(F32)
-        pg[k, rows_of(me_t), :] = (total * (1.0 - c * c)).astype(BF16)
+        pg[k, rows_of(z, T), :] = (total * (1.0 - c * c)).astype(BF16)
         if Z > 1:
-            relay(me_t, k, 0, me_t + 2, has_r)
-            relay(me_t, k, 1, me_t - 2, has_l)
-        relay(me_t, k, 2, ypart)
+            relay(z, k, 0, has_r)
+            relay(z, k, 1, has_l)
 
     def hid_part(s):
         total = jnp.zeros((T, E), F32)
         for k in range(K):
             total = total + lax.dot_general(
-                pg[k, rows_of(me_t), :], w[k, pl.ds(pl.multiple_of(s * E, E), E), :], NT,
+                pg[k, rows_of(z, T), :], w[k, pl.ds(pl.multiple_of(s * E, E), E), :], NT,
                 preferred_element_type=F32)
         return total
 
@@ -219,47 +214,60 @@
         send(hss.at[d], hsr.at[d], hs_s.at[d], hs_r.at[d], {"voc": s})
     own_hs[...] = hid_part(me_v)
 
-    for d in range(1, M):
-        src = lax.rem(me_t - d + M, M)
-        arrived(hrow.at[pl.ds(src * T, T)], hid_r.at[d], hid_s.at[d])
-
-    def pair(zz, first=False):
-        t = zz * 2 + 1 - y
-        both = pl.ds(pl.multiple_of(zz * 2 * T, 2 * T), 2 * T)
-        left = hrow[both, :].T
-        for k in range(K):
-            arrived(pg.at[k, rows_of(t)], ag_r.at[t, k], ag_s.at[2, t, k])
-            part = jnp.dot(left, pg[k, both, :], preferred_element_type=F32)
-            acc[k] = part if first else acc[k] + part
-
-    def pairs(d):
-        if d == 0:
-            pair(z, True)
-        else:
-            pl.when(z >= d)(lambda: pair(z - d))
-            pl.when(z + d < Z)(lambda: pair(z + d))
+    for zz in range(Z):
+        arrived(vgy.at[zz], vy_r.at[zz], vy_s.at[zz])
+        vsum[zz] = vgb[rows_of(zz * 2 + y, R), :].astype(F32) + vgy[zz].astype(F32)
+
+    def hop(h):
+        for way, at, ends in ((0, h, range(h + 1, Z)), (1, Z - 1 - h, range(Z - 1 - h))):
+            copies = [
+                remote(vout.at[way, e], vin.at[way, e], vz_s.at[way, e], vz_r.at[way, e],
+                       {"tok": me_t + 2 - 4 * way})
+                for e in ends
+            ]
+
+            @pl.when(z == at)
+            def _(way=way, ends=ends, copies=copies):
+                for e, c in zip(ends, copies):
+                    part = vsum[e]
+                    if h > 0:
+                        arrived(vin.at[way, e], vz_r.at[way, e], vz_s.at[way, e])
+                        part = part + vin[way, e].astype(F32)
+                    vout[way, e] = part.astype(BF16)
+                    c.start()
+            for c in copies:
+                sends.append((z == at, c))
 
     for d in range(1, Z):
-        from_l = z >= d
-        from_r = z + d < Z
-        for k in range(K):
-            for there, t, way, dev, more in (
-                (from_l, me_t - 2 * d, 0, me_t + 2, has_r),
-                (from_r, me_t + 2 * d, 1, me_t - 2, has_l),
+        src = lax.rem(z - d + Z, Z)
+        arrived(hrow.at[:, pl.ds(src * T, T)], hid_r.at[d], hid_s.at[d])
+    for b in range(2):
+        htr[b] = hrow[b].T
+
+    per = pl.cdiv(max(Z - 1, 1), K)
+    for k in range(K):
+        for h in range(k * per, min((k + 1) * per, Z - 1)):
+            hop(h)
+        for d in range(1, Z):
+            for there, t, way, more in (
+                (z >= d, z - d, 0, has_r), (z + d < Z, z + d, 1, has_l),
             ):
                 def _(t=t, k=k):
-                    arrived(pg.at[k, rows_of(t)], ag_r.at[t, k], ag_s.at[2, t, k])
+                    arrived(pg.at[k, rows_of(t, T)], ag_r.at[t, k], ag_s.at[0, t, k])
                 pl.when(there)(_)
                 if d < Z - 1:
-                    relay(t, k, way, dev, there & more)
-                relay(t, k, 2, ypart, there)
-        pairs(d - 1)
-
-    vtot = vgb[rows_r(me_t, R), :].astype(F32)
-    for d in range(1, M):
-        arrived(vgr.at[d], vg_r.at[d], vg_s.at[d])
-        vtot = vtot + vgr[d].astype(F32)
-    out_vocab[...] = vtot.astype(BF16)
+                    relay(t, k, way, there & more)
+        psend[k] = jnp.dot(htr[1 - y], pg[k], preferred_element_type=F32).astype(BF16)
+        send(psend.at[k], precv.at[k], pp_s.at[k], pp_r.at[k], {"tok": ypart})
+        acc[k] = jnp.dot(htr[y], pg[k], preferred_element_type=F32)
+
+    acc_v = vsum.at[z]
+    for way, pred in ((0, has_l), (1, has_r)):
+        @pl.when(pred)
+        def _(way=way):
+            arrived(vin.at[way, z], vz_r.at[way, z], vz_s.at[way, z])
+            acc_v[...] += vin[way, z].astype(F32)
+    out_vocab[...] = acc_v[...].astype(BF16)
     htot = own_hs[...]
     for d in range(1, N):
         arrived(hsr.at[d], hs_r.at[d], hs_s.at[d])
@@ -269,9 +277,9 @@
         htot = htot + column(mgrad[k:k + 1, :], E) * mixf[k:k + 1, :]
     out_hidden[...] = htot.astype(BF16)
 
-    pairs(Z - 1)
-    for k in range(K):
-        out_proj[k] = acc[k].astype(BF16)
+    for k in range(K):
+        arrived(precv.at[k], pp_r.at[k], pp_s.at[k])
+        out_proj[k] = (acc[k] + precv[k].astype(F32)).astype(BF16)
     for pred, c in sends:
         if pred is None:
             c.wait_send()
@@ -279,8 +287,8 @@
             pl.when(pred)(c.wait_send)
 
 
-def rows_r(t, R):
-    return pl.ds(pl.multiple_of(t * R, R), R)
+def rows_of(block, size):
+    return pl.ds(pl.multiple_of(block * size, size), size)
 
 
 def body(M, N, hidden, mix_weight, comp_proj, vocab_weight, log_normalizer, targets, loss_grad):
@@ -289,22 +297,26 @@
     V = vocab_weight.shape[1]
     R = D // M
     half = N // 2
+    Z = M // 2
     w = jnp.transpose(comp_proj, (1, 0, 2))
     vm = pltpu.VMEM
     dma = pltpu.SemaphoreType.DMA
     scratch = [
         vm((K, D, E), BF16), vm((N, K * T, E), BF16), vm((N, K, E), BF16),
-        vm((M, T, R), BF16), vm((M * T, R), BF16), vm((K * T, V), F32), vm((K * T, V), BF16),
+        vm((Z, 2, T, R), BF16), vm((2, Z * T, R), BF16), vm((2, R, Z * T), BF16), vm((K * T, V), F32), vm((K * T, V), BF16),
         vm((N, 8, T), F32),
         vm((half, K, T, E), BF16), vm((half, K, T, E), BF16),
         vm((half, K, T, E), BF16), vm((half, K, T, E), BF16),
-        vm((K, T, E), F32), vm((D, V), BF16), vm((M, R, V), BF16),
-        vm((K, M * T, E), BF16), vm((N, T, E), BF16), vm((N, T, E), BF16),
-        vm((T, E), F32), vm((K, R, E), F32), vm((K, T), F32),
+        vm((K, T, E), F32), vm((D, V), BF16), vm((Z, R, V), BF16),
+        vm((Z, R, V), F32), vm((2, Z, R, V), BF16), vm((2, Z, R, V), BF16),
+        vm((K, Z * T, E), BF16), vm((N, T, E), BF16), vm((N, T, E), BF16),
+        vm((T, E), F32), vm((K, R, E), F32), vm((K, R, E), BF16), vm((K, R, E), BF16),
+        vm((K, T), F32),
         dma((K,)), dma((half, K)), dma((half, K)), dma((N, K)), dma((N,)), dma((N,)),
-        dma((M,)), dma((M,)), dma((N,)), dma((N,)),
+        dma((Z,)), dma((Z,)), dma((N,)), dma((N,)),
         dma((half, K)), dma((half, K)), dma((half, K)), dma((half, K)),
-        dma((M,)), dma((M,)), dma((N,)), dma((N,)), dma((3, M, K)), dma((M, K)),
+        dma((Z,)), dma((Z,)), dma((2, Z)), dma((2, Z)), dma((N,)), dma((N,)),
+        dma((2, Z, K)), dma((Z, K)), dma((K,)), dma((K,)),
     ]
     spec = pl.BlockSpec(memory_space=pltpu.VMEM)
     hidden_grad, proj_grad, vocab_grad = pl.pallas_call(
@@ -314,11 +326,11 @@
             jax.ShapeDtypeStruct((K, R, E), BF16),
             jax.ShapeDtypeStruct((R, V), BF16),
         ),
-        in_specs=[spec, spec, pl.BlockSpec(memory_space=pl.ANY), spec, spec, spec, spec],
+        in_specs=[spec, spec, pl.BlockSpec(memory_space=pltpu.MemorySpace.HBM)] + [spec] * 4,
         out_specs=(spec, spec, spec),
         scratch_shapes=scratch,
         compiler_params=pltpu.CompilerParams(
-            collective_id=0, has_side_effects=True, vmem_limit_bytes=56 * 1024 * 1024
+            collective_id=0, has_side_effects=True, vmem_limit_bytes=48 * 1024 * 1024
         ),
     )(hidden, mix_weight, w, vocab_weight, log_normalizer, targets[None, :], loss_grad[None, :])
     return hidden_grad, jnp.transpose(proj_grad, (1, 0, 2)), vocab_grad

time: 108 us -> 96.5 us (0.89)
  the two profiles are of different devices: /device:TPU:16 before, /device:TPU:0 now
where the time goes in v2:
time: 96.5 us; the launch traced here: 96.3 us
  Pallas kernels  84 us (87%)
  local copies, waits for them, and re-layouts  11.5 us (12%)
    pallas_call x1, Pallas kernels, body(): pl.pallas_call(functools.partial(kernel, M, N), out_shape=(jax.ShapeDtype...  84 us
    unnamed x16, local copies, waits for them, and re-layouts  11.5 us

profile of v2, /device:TPU:0, one launch (start us, length us, event | category | flops | bytes accessed | tf_op | source)
XLA Modules:
  0.0 96.3 jit_solution(16827291014110834965)
XLA Ops:
  0.6 0.0 copy-start
  0.6 0.0 copy-start.1
  0.7 0.0 copy-start.2
  0.7 0.0 copy-start.3
  0.7 0.0 copy-start.4
  0.7 0.0 copy-start.5
  0.7 8.4 %copy.13 = bf16[2048,4,512]{2,0,1:T(8,128)(2,1)} copy(bf16[2048,4,512]{2,1,0:T(4,128)(2,1)} %param.9) | data formatting | bytes 16777216 | tf_op args[2]
  9.1 0.0 copy-done
  9.1 0.0 copy-done.1
  9.1 0.0 copy-done.2
  9.1 0.0 copy-done.3
  9.1 0.0 copy-done.4
  9.1 0.0 copy-done.5
  9.1 84.0 %shard_map.94 = (bf16[128,512]{1,0:T(8,128)(2,1)S(1)}, bf16[4,256,512]{2,1,0:T(8,128)(2,1)S(1)}, bf16[256,256]{1,0:T(8,128)(2,1)S(1)}) custom-call(bf16[128,2048]{1,0:T(8,128)(2,1)S(1)} %copy-done.1, bf16[4,512]{1,0:T(4,128)(2,1)S(1)} %copy-done.2, bf16[4,2048,512]{2,1,0:T(8,128)(2,1)} %bitcast.9, bf16[2048,256]{1,0:T(8,128)(2,1)S(1)} %copy-done, ...), custom_call_target="tpu_custom_call" | custom-call | tf_op jit(solution)/shard_map/pallas_call | solution.py:322
  93.2 1.8 %copy.11 = bf16[256,4,512]{2,1,0:T(4,128)(2,1)} copy(bf16[256,4,512]{2,0,1:T(8,128)(2,1)S(1)} %bitcast.6) | data formatting | bytes 2097152
  95.0 0.7 copy.16
  95.6 0.7 copy.17
Async XLA Ops:
  0.6 8.5 %copy-start = (bf16[2048,256]{1,0:T(8,128)(2,1)S(1)}, bf16[2048,256]{1,0:T(8,128)(2,1)}, u32[]{:S(2)}) copy-start(bf16[2048,256]{1,0:T(8,128)(2,1)} %vw.1) | copy-start | bytes 3145732
  0.6 8.5 %copy-start.1 = (bf16[128,2048]{1,0:T(8,128)(2,1)S(1)}, bf16[128,2048]{1,0:T(8,128)(2,1)}, u32[]{:S(2)}) copy-start(bf16[128,2048]{1,0:T(8,128)(2,1)} %hidden.1) | copy-start | bytes 1572868
  0.7 8.5 %copy-start.2 = (bf16[4,512]{1,0:T(4,128)(2,1)S(1)}, bf16[4,512]{1,0:T(4,128)(2,1)}, u32[]{:S(2)}) copy-start(bf16[4,512]{1,0:T(4,128)(2,1)} %mix.1) | copy-start | bytes 12292
  0.7 8.5 %copy-start.3 = (f32[4,128]{1,0:T(4,128)S(1)}, f32[4,128]{1,0:T(4,128)}, u32[]{:S(2)}) copy-start(f32[4,128]{1,0:T(4,128)} %logz.1) | copy-start | bytes 6148
  0.7 8.5 %copy-start.4 = (s32[128]{0:T(128)S(1)}, s32[128]{0:T(128)}, u32[]{:S(2)}) copy-start(s32[128]{0:T(128)} %param.12) | copy-start | bytes 1540
  0.7 8.5 %copy-start.5 = (f32[128]{0:T(128)S(1)}, f32[128]{0:T(128)}, u32[]{:S(2)}) copy-start(f32[128]{0:T(128)} %param.13) | copy-start | bytes 1540

commit v3 on v2

--- a/solution.py
+++ b/solution.py
@@ -34,6 +34,9 @@
     R = D // M
     half = N // 2
     Z = M // 2
+    H = 2
+    TH = T // H
+    Q = K * TH // T
     me_t = lax.axis_index("tok")
     me_v = lax.axis_index("voc")
     chip = me_v // 2
@@ -79,26 +82,37 @@
              {"tok": zz * 2 + y})
     hrow[:, rows_of(z, T), :] = hblk[z]
 
+    def send_context(h, k):
+        piece = ctx.at[me_v, h, pl.ds(k * TH, TH)]
+        for i in range(1, half):
+            send(piece, piece, ctx_s.at[i, h, k], ctx_r.at[me_v, h, k],
+                 {"voc": lax.rem(chip + i, half) * 2 + core})
+        send(piece, piece, ctx_s.at[0, h, k], ctx_r.at[me_v, h, k], {"voc": partner})
+
     for k in range(K):
         pltpu.make_async_copy(proj_hbm.at[k], w.at[k], w_sem.at[k]).wait()
-        ctx[me_v, k * T:(k + 1) * T, :] = jnp.tanh(
+        own = jnp.tanh(
             jnp.dot(hidden[...], w[k], preferred_element_type=F32)
         ).astype(BF16)
-        piece = ctx.at[me_v, pl.ds(k * T, T)]
-        for i in range(1, half):
-            send(piece, piece, ctx_s.at[i, k], ctx_r.at[me_v, k],
-                 {"voc": lax.rem(chip + i, half) * 2 + core})
-        send(piece, piece, ctx_s.at[0, k], ctx_r.at[me_v, k], {"voc": partner})
-
-    def add_logits(s, first=False):
-        part = jnp.dot(ctx[s], vw[pl.ds(pl.multiple_of(s * E, E), E), :],
+        for h in range(H):
+            ctx[me_v, h, k * TH:(k + 1) * TH, :] = own[h * TH:(h + 1) * TH]
+        send_context(0, k)
+    for h in range(1, H):
+        for k in range(K):
+            send_context(h, k)
+
+    def add_logits(s, h, first=False):
+        part = jnp.dot(ctx[s, h], vw[pl.ds(pl.multiple_of(s * E, E), E), :],
                        preferred_element_type=F32)
-        logit[...] = part if first else logit[...] + part
-
-    add_logits(me_v, True)
-    for k in range(K):
-        arrived(ctx.at[partner, pl.ds(k * T, T)], ctx_r.at[partner, k], ctx_s.at[0, k])
-    add_logits(partner)
+        logit[h] = part if first else logit[h] + part
+
+    def near_logits(h):
+        add_logits(me_v, h, True)
+        for k in range(K):
+            arrived(ctx.at[partner, h, pl.ds(k * TH, TH)], ctx_r.at[partner, h, k], ctx_s.at[0, h, k])
+        add_logits(partner, h)
+
+    near_logits(0)
 
     tcol = column(targets[...].astype(F32), V)
     ids = (me_v * V + lax.broadcasted_iota(jnp.int32, (T, V), 1)).astype(F32)
@@ -114,91 +128,119 @@
     exp_mix = jnp.exp(mixing)
     weights = exp_mix / jnp.sum(exp_mix, axis=0, keepdims=True)
 
-    for i in range(1, half):
-        s = lax.rem(chip - i + half, half) * 2 + core
-        for k in range(K):
-            piece = ctx.at[s, pl.ds(k * T, T)]
-            arrived(piece, ctx_r.at[s, k], ctx_s.at[i, k])
-            send(piece, piece, ctx_f.at[i, k], ctx_r.at[s, k], {"voc": partner})
-        add_logits(s)
-    for i in range(1, half):
-        s = lax.rem(chip - i + half, half) * 2 + 1 - core
-        for k in range(K):
-            arrived(ctx.at[s, pl.ds(k * T, T)], ctx_r.at[s, k], ctx_s.at[i, k])
-        add_logits(s)
-
-    lane = lax.broadcasted_iota(jnp.int32, (T, 128), 1)
-    table = jnp.zeros((T, 128), F32)
-    for k in range(K):
-        part = jnp.sum(logit[k * T:(k + 1) * T, :] * onehot, axis=1, keepdims=True)
-        table = jnp.where(lane == k, part, table)
-    tgt[0] = table.T[0:8, :]
-    for d in range(1, N):
-        send(tgt.at[0], tgt.at[d], tgt_s.at[d], tgt_r.at[d], {"voc": lax.rem(me_v + d, N)})
-    for k in range(K):
-        rows = slice(k * T, (k + 1) * T)
-        logit[rows, :] = jnp.exp(logit[rows, :] - column(logz[k:k + 1, :], V)) - onehot
-    for d in range(1, N):
-        arrived(tgt.at[d], tgt_r.at[d], tgt_s.at[d])
-    target = tgt[0]
-    for d in range(1, N):
-        target = target + tgt[d]
-    likely = jnp.exp(target[0:K, :] - logz[...])
-    joint = weights * likely
-    posterior = joint / jnp.sum(joint, axis=0, keepdims=True)
-    factor = loss[...] * posterior
-    mgrad[...] = loss[...] * (weights - posterior)
-    for k in range(K):
-        rows = slice(k * T, (k + 1) * T)
-        lg[rows, :] = (column(factor[k:k + 1, :], V) * logit[rows, :]).astype(BF16)
-
-    def cg_part(s, k):
+    lane = lax.broadcasted_iota(jnp.int32, (TH, 128), 1)
+    norm = [column(logz[k:k + 1, :], V) for k in range(K)]
+
+    def cut(k):
+        return slice(k * TH, (k + 1) * TH)
+
+    def far_logits(h):
+        for i in range(1, half):
+            s = lax.rem(chip - i + half, half) * 2 + core
+            for k in range(K):
+                piece = ctx.at[s, h, pl.ds(k * TH, TH)]
+                arrived(piece, ctx_r.at[s, h, k], ctx_s.at[i, h, k])
+                send(piece, piece, ctx_f.at[i, h, k], ctx_r.at[s, h, k], {"voc": partner})
+            add_logits(s, h)
+        for i in range(1, half):
+            s = lax.rem(chip - i + half, half) * 2 + 1 - core
+            for k in range(K):
+                arrived(ctx.at[s, h, pl.ds(k * TH, TH)], ctx_r.at[s, h, k], ctx_s.at[i, h, k])
+            add_logits(s, h)
+        table = jnp.zeros((TH, 128), F32)
+        for k in range(K):
+            part = jnp.sum(logit[h, cut(k), :] * onehot[cut(h)], axis=1, keepdims=True)
+            table = jnp.where(lane == k, part, table)
+        zero = jnp.zeros((TH, 128), F32)
+        tgt[h, 0] = jnp.concatenate([table if g == h else zero for g in range(H)], axis=0).T[0:8, :]
+        for d in range(1, N):
+            send(tgt.at[h, 0], tgt.at[h, d], tgt_s.at[h, d], tgt_r.at[h, d],
+                 {"voc": lax.rem(me_v + d, N)})
+        for k in range(K):
+            logit[h, cut(k), :] = jnp.exp(logit[h, cut(k), :] - norm[k][cut(h)]) - onehot[cut(h)]
+
+    def cg_part(s, h, q):
         return lax.dot_general(
-            lg[k * T:(k + 1) * T, :], vw[pl.ds(pl.multiple_of(s * E, E), E), :], NT,
+            lg[h, q * T:(q + 1) * T, :], vw[pl.ds(pl.multiple_of(s * E, E), E), :], NT,
             preferred_element_type=F32)
 
-    for i in list(range(1, half)) + [0]:
-        s = lax.rem(chip + i, half) * 2
-        for k in range(K):
-            cgs[i, k] = cg_part(s + 1 - core, k).astype(BF16)
-            send(cgs.at[i, k], cgr.at[i, k], cgp_s.at[i, k], cgp_r.at[i, k], {"voc": partner})
-        for k in range(K):
-            part = cg_part(s + core, k)
-            if i == 0:
-                own_cg[k] = part
-            else:
-                arrived(cgr.at[i, k], cgp_r.at[i, k], cgp_s.at[i, k])
-                cgx[i, k] = (part + cgr[i, k].astype(F32)).astype(BF16)
-                send(cgx.at[i, k], xr.at[i, k], cgx_s.at[i, k], cgx_r.at[i, k], {"voc": s + core})
+    def gradients(h):
+        for d in range(1, N):
+            arrived(tgt.at[h, d], tgt_r.at[h, d], tgt_s.at[h, d])
+        target = tgt[h, 0]
+        for d in range(1, N):
+            target = target + tgt[h, d]
+        likely = jnp.exp(target[0:K, :] - logz[...])
+        joint = weights * likely
+        posterior = joint / jnp.sum(joint, axis=0, keepdims=True)
+        factor = loss[...] * posterior
+        slope = loss[...] * (weights - posterior)
+        token = lax.broadcasted_iota(jnp.int32, (K, T), 1)
+        mgrad[...] = slope if h == 0 else jnp.where(token >= h * TH, slope, mgrad[...])
+        for k in range(K):
+            lg[h, cut(k), :] = (
+                column(factor[k:k + 1, :], V)[cut(h)] * logit[h, cut(k), :]).astype(BF16)
+        for i in list(range(1, half)) + [0]:
+            s = lax.rem(chip + i, half) * 2
+            for q in range(Q):
+                cgs[i, h, q] = cg_part(s + 1 - core, h, q).astype(BF16)
+                send(cgs.at[i, h, q], cgr.at[i, h, q], cgp_s.at[i, h, q], cgp_r.at[i, h, q],
+                     {"voc": partner})
+            for q in range(Q):
+                part = cg_part(s + core, h, q)
+                if i == 0:
+                    own_cg[h, q] = part
+                else:
+                    arrived(cgr.at[i, h, q], cgp_r.at[i, h, q], cgp_s.at[i, h, q])
+                    cgx[i, h, q] = (part + cgr[i, h, q].astype(F32)).astype(BF16)
+                    send(cgx.at[i, h, q], xr.at[i, h, q], cgx_s.at[i, h, q], cgx_r.at[i, h, q],
+                         {"voc": s + core})
+
+    far_logits(0)
+    near_logits(1)
+    gradients(0)
+    far_logits(1)
+    gradients(1)
 
     for s in range(N):
-        vgb[s * E:(s + 1) * E, :] = lax.dot_general(
-            ctx[s], lg[...], TN, preferred_element_type=F32).astype(BF16)
+        vgb[s * E:(s + 1) * E, :] = sum(
+            lax.dot_general(ctx[s, h], lg[h], TN, preferred_element_type=F32) for h in range(H)
+        ).astype(BF16)
     for zz in range(Z):
         send(vgb.at[pl.ds((zz * 2 + 1 - y) * R, R)], vgy.at[zz], vy_s.at[zz], vy_r.at[zz],
              {"tok": ypart})
 
-    def relay(t, k, way, pred):
-        piece = pg.at[k, rows_of(t, T)]
-        c = remote(piece, piece, ag_s.at[way, t, k], ag_r.at[t, k],
+    pieces = [(k, 0, E) for k in range(K)]
+    if E % 256 == 0:
+        pieces[-1:] = [(K - 1, 0, E // 2), (K - 1, E // 2, E // 2)]
+
+    def relay(t, p, way, pred, h=None):
+        k, lo, wide = pieces[p]
+        rows = rows_of(t, T) if h is None else rows_of(t * H + h, TH)
+        piece = pg.at[k, rows, pl.ds(lo, wide)]
+        c = remote(piece, piece, ag_s.at[way, t, p, 0 if h is None else h], ag_r.at[t, p],
                    {"tok": me_t + 2 - 4 * way})
         pl.when(pred)(c.start)
         sends.append((pred, c))
 
     has_r = z + 1 < Z
     has_l = z >= 1
-    for k in range(K):
-        total = own_cg[k]
-        arrived(cgr.at[0, k], cgp_r.at[0, k], cgp_s.at[0, k])
-        total = total + cgr[0, k].astype(F32)
-        for i in range(1, half):
-            arrived(xr.at[i, k], cgx_r.at[i, k], cgx_s.at[i, k])
-            total = total + xr[i, k].astype(F32)
-        c = ctx[me_v, k * T:(k + 1) * T, :].astype(F32)
-        pg[k, rows_of(z, T), :] = (total * (1.0 - c * c)).astype(BF16)
-        if Z > 1:
-            relay(z, k, 0, has_r)
-            relay(z, k, 1, has_l)
+    for h in range(H):
+        for q in range(Q):
+            arrived(cgr.at[0, h, q], cgp_r.at[0, h, q], cgp_s.at[0, h, q])
+            total = own_cg[h, q] + cgr[0, h, q].astype(F32)
+            for i in range(1, half):
+                arrived(xr.at[i, h, q], cgx_r.at[i, h, q], cgx_s.at[i, h, q])
+                total = total + xr[i, h, q].astype(F32)
+            c = ctx[me_v, h, q * T:(q + 1) * T, :].astype(F32)
+            grad = (total * (1.0 - c * c)).astype(BF16)
+            for g in range(H):
+                pg[q * H + g, rows_of(z * H + h, TH), :] = grad[g * TH:(g + 1) * TH]
+            if Z > 1:
+                for p, (k, lo, wide) in enumerate(pieces):
+                    if k // H == q:
+                        relay(z, p, 0, has_r, h)
+                        relay(z, p, 1, has_l, h)
 
     def hid_part(s):
         total = jnp.zeros((T, E), F32)
@@ -245,21 +287,24 @@
         htr[b] = hrow[b].T
 
     per = pl.cdiv(max(Z - 1, 1), K)
-    for k in range(K):
-        for h in range(k * per, min((k + 1) * per, Z - 1)):
+    for p, (k, lo, wide) in enumerate(pieces):
+        lanes = slice(lo, lo + wide)
+        for h in range(p * per, min((p + 1) * per, Z - 1)):
             hop(h)
         for d in range(1, Z):
             for there, t, way, more in (
                 (z >= d, z - d, 0, has_r), (z + d < Z, z + d, 1, has_l),
             ):
-                def _(t=t, k=k):
-                    arrived(pg.at[k, rows_of(t, T)], ag_r.at[t, k], ag_s.at[0, t, k])
+                def _(t=t):
+                    arrived(pg.at[k, rows_of(t, T), pl.ds(lo, wide)], ag_r.at[t, p], ag_s.at[0, t, p, 0])
                 pl.when(there)(_)
                 if d < Z - 1:
-                    relay(t, k, way, there & more)
-        psend[k] = jnp.dot(htr[1 - y], pg[k], preferred_element_type=F32).astype(BF16)
-        send(psend.at[k], precv.at[k], pp_s.at[k], pp_r.at[k], {"tok": ypart})
-        acc[k] = jnp.dot(htr[y], pg[k], preferred_element_type=F32)
+                    relay(t, p, way, there & more)
+        psend[k, :, lanes] = jnp.dot(
+            htr[1 - y], pg[k, :, lanes], preferred_element_type=F32).astype(BF16)
+        send(psend.at[k, :, pl.ds(lo, wide)], precv.at[k, :, pl.ds(lo, wide)],
+             pp_s.at[p], pp_r.at[p], {"tok": ypart})
+        acc[k, :, lanes] = jnp.dot(htr[y], pg[k, :, lanes], preferred_element_type=F32)
 
     acc_v = vsum.at[z]
     for way, pred in ((0, has_l), (1, has_r)):
@@ -277,9 +322,10 @@
         htot = htot + column(mgrad[k:k + 1, :], E) * mixf[k:k + 1, :]
     out_hidden[...] = htot.astype(BF16)
 
-    for k in range(K):
-        arrived(precv.at[k], pp_r.at[k], pp_s.at[k])
-        out_proj[k] = (acc[k] + precv[k].astype(F32)).astype(BF16)
+    for p, (k, lo, wide) in enumerate(pieces):
+        lanes = slice(lo, lo + wide)
+        arrived(precv.at[k, :, pl.ds(lo, wide)], pp_r.at[p], pp_s.at[p])
+        out_proj[k, :, lanes] = (acc[k, :, lanes] + precv[k, :, lanes].astype(F32)).astype(BF16)
     for pred, c in sends:
         if pred is None:
             c.wait_send()
@@ -298,25 +344,28 @@
     R = D // M
     half = N // 2
     Z = M // 2
+    H = 2
+    TH = T // H
+    Q = K * TH // T
     w = jnp.transpose(comp_proj, (1, 0, 2))
     vm = pltpu.VMEM
     dma = pltpu.SemaphoreType.DMA
     scratch = [
-        vm((K, D, E), BF16), vm((N, K * T, E), BF16), vm((N, K, E), BF16),
-        vm((Z, 2, T, R), BF16), vm((2, Z * T, R), BF16), vm((2, R, Z * T), BF16), vm((K * T, V), F32), vm((K * T, V), BF16),
-        vm((N, 8, T), F32),
-        vm((half, K, T, E), BF16), vm((half, K, T, E), BF16),
-        vm((half, K, T, E), BF16), vm((half, K, T, E), BF16),
-        vm((K, T, E), F32), vm((D, V), BF16), vm((Z, R, V), BF16),
+        vm((K, D, E), BF16), vm((N, H, K * TH, E), BF16), vm((N, K, E), BF16),
+        vm((Z, 2, T, R), BF16), vm((2, Z * T, R), BF16), vm((2, R, Z * T), BF16), vm((H, K * TH, V), F32), vm((H, K * TH, V), BF16),
+        vm((H, N, 8, T), F32),
+        vm((half, H, Q, T, E), BF16), vm((half, H, Q, T, E), BF16),
+        vm((half, H, Q, T, E), BF16), vm((half, H, Q, T, E), BF16),
+        vm((H, Q, T, E), F32), vm((D, V), BF16), vm((Z, R, V), BF16),
         vm((Z, R, V), F32), vm((2, Z, R, V), BF16), vm((2, Z, R, V), BF16),
         vm((K, Z * T, E), BF16), vm((N, T, E), BF16), vm((N, T, E), BF16),
         vm((T, E), F32), vm((K, R, E), F32), vm((K, R, E), BF16), vm((K, R, E), BF16),
         vm((K, T), F32),
-        dma((K,)), dma((half, K)), dma((half, K)), dma((N, K)), dma((N,)), dma((N,)),
-        dma((Z,)), dma((Z,)), dma((N,)), dma((N,)),
-        dma((half, K)), dma((half, K)), dma((half, K)), dma((half, K)),
+        dma((K,)), dma((half, H, K)), dma((half, H, K)), dma((N, H, K)), dma((N,)), dma((N,)),
+        dma((Z,)), dma((Z,)), dma((H, N)), dma((H, N)),
+        dma((half, H, Q)), dma((half, H, Q)), dma((half, H, Q)), dma((half, H, Q)),
         dma((Z,)), dma((Z,)), dma((2, Z)), dma((2, Z)), dma((N,)), dma((N,)),
-        dma((2, Z, K)), dma((Z, K)), dma((K,)), dma((K,)),
+        dma((2, Z, K + 1, H)), dma((Z, K + 1)), dma((K + 1,)), dma((K + 1,)),
     ]
     spec = pl.BlockSpec(memory_space=pltpu.VMEM)
     hidden_grad, proj_grad, vocab_grad = pl.pallas_call(

time: 96.5 us -> 99.9 us (1.035)
  Pallas kernels: 84 us -> 87.5 us
    pallas_call x1, Pallas kernels: 84 us -> 87.5 us  [body(): pl.pallas_call(functools.partial(kernel, M, N), out_shape=(jax.ShapeDtype...]
where the time goes in v3:
time: 99.9 us; the launch traced here: 99.7 us
  Pallas kernels  87.5 us (88%)
  local copies, waits for them, and re-layouts  11.5 us (12%)
    pallas_call x1, Pallas kernels, body(): pl.pallas_call(functools.partial(kernel, M, N), out_shape=(jax.ShapeDtype...  87.5 us
    unnamed x16, local copies, waits for them, and re-layouts  11.5 us

profile of v3, /device:TPU:0, one launch (start us, length us, event | category | flops | bytes accessed | tf_op | source)
XLA Modules:
  0.0 99.7 jit_solution(14305711903014881374)
XLA Ops:
  0.6 0.0 copy-start
  0.6 0.0 copy-start.1
  0.7 0.0 copy-start.2
  0.7 0.0 copy-start.3
  0.7 0.0 copy-start.4
  0.7 0.0 copy-start.5
  0.7 8.4 %copy.13 = bf16[2048,4,512]{2,0,1:T(8,128)(2,1)} copy(bf16[2048,4,512]{2,1,0:T(4,128)(2,1)} %param.9) | data formatting | bytes 16777216 | tf_op args[2]
  9.1 0.0 copy-done
  9.1 0.0 copy-done.1
  9.1 0.0 copy-done.2
  9.1 0.0 copy-done.3
  9.1 0.0 copy-done.4
  9.1 0.0 copy-done.5
  9.1 87.5 %shard_map.94 = (bf16[128,512]{1,0:T(8,128)(2,1)S(1)}, bf16[4,256,512]{2,1,0:T(8,128)(2,1)S(1)}, bf16[256,256]{1,0:T(8,128)(2,1)S(1)}) custom-call(bf16[128,2048]{1,0:T(8,128)(2,1)S(1)} %copy-done.1, bf16[4,512]{1,0:T(4,128)(2,1)S(1)} %copy-done.2, bf16[4,2048,512]{2,1,0:T(8,128)(2,1)} %bitcast.9, bf16[2048,256]{1,0:T(8,128)(2,1)S(1)} %copy-done, ...), custom_call_target="tpu_custom_call" | custom-call | tf_op jit(solution)/shard_map/pallas_call | solution.py:371
  96.6 1.8 %copy.11 = bf16[256,4,512]{2,1,0:T(4,128)(2,1)} copy(bf16[256,4,512]{2,0,1:T(8,128)(2,1)S(1)} %bitcast.6) | data formatting | bytes 2097152
  98.4 0.7 copy.16
  99.0 0.7 copy.17
Async XLA Ops:
  0.6 8.5 %copy-start = (bf16[2048,256]{1,0:T(8,128)(2,1)S(1)}, bf16[2048,256]{1,0:T(8,128)(2,1)}, u32[]{:S(2)}) copy-start(bf16[2048,256]{1,0:T(8,128)(2,1)} %vw.1) | copy-start | bytes 3145732
  0.6 8.5 %copy-start.1 = (bf16[128,2048]{1,0:T(8,128)(2,1)S(1)}, bf16[128,2048]{1,0:T(8,128)(2,1)}, u32[]{:S(2)}) copy-start(bf16[128,2048]{1,0:T(8,128)(2,1)} %hidden.1) | copy-start | bytes 1572868
  0.7 8.5 %copy-start.2 = (bf16[4,512]{1,0:T(4,128)(2,1)S(1)}, bf16[4,512]{1,0:T(4,128)(2,1)}, u32[]{:S(2)}) copy-start(bf16[4,512]{1,0:T(4,128)(2,1)} %mix.1) | copy-start | bytes 12292
  0.7 8.5 %copy-start.3 = (f32[4,128]{1,0:T(4,128)S(1)}, f32[4,128]{1,0:T(4,128)}, u32[]{:S(2)}) copy-start(f32[4,128]{1,0:T(4,128)} %logz.1) | copy-start | bytes 6148
  0.7 8.5 %copy-start.4 = (s32[128]{0:T(128)S(1)}, s32[128]{0:T(128)}, u32[]{:S(2)}) copy-start(s32[128]{0:T(128)} %param.12) | copy-start | bytes 1540
  0.7 8.5 %copy-start.5 = (f32[128]{0:T(128)S(1)}, f32[128]{0:T(128)}, u32[]{:S(2)}) copy-start(f32[128]{0:T(128)} %param.13) | copy-start | bytes 1540

commit v4 on v2

--- a/solution.py
+++ b/solution.py
@@ -178,9 +178,20 @@
         send(vgb.at[pl.ds((zz * 2 + 1 - y) * R, R)], vgy.at[zz], vy_s.at[zz], vy_r.at[zz],
              {"tok": ypart})
 
-    def relay(t, k, way, pred):
-        piece = pg.at[k, rows_of(t, T)]
-        c = remote(piece, piece, ag_s.at[way, t, k], ag_r.at[t, k],
+    for d in range(1, Z):
+        src = lax.rem(z - d + Z, Z)
+        arrived(hrow.at[:, pl.ds(src * T, T)], hid_r.at[d], hid_s.at[d])
+    for b in range(2):
+        htr[b] = hrow[b].T
+
+    pieces = [(k, 0, E) for k in range(K)]
+    if E % 256 == 0:
+        pieces[-1:] = [(K - 1, 0, E // 2), (K - 1, E // 2, E // 2)]
+
+    def relay(t, p, way, pred):
+        k, lo, wide = pieces[p]
+        piece = pg.at[k, rows_of(t, T), pl.ds(lo, wide)]
+        c = remote(piece, piece, ag_s.at[way, t, p], ag_r.at[t, p],
                    {"tok": me_t + 2 - 4 * way})
         pl.when(pred)(c.start)
         sends.append((pred, c))
@@ -197,8 +208,10 @@
         c = ctx[me_v, k * T:(k + 1) * T, :].astype(F32)
         pg[k, rows_of(z, T), :] = (total * (1.0 - c * c)).astype(BF16)
         if Z > 1:
-            relay(z, k, 0, has_r)
-            relay(z, k, 1, has_l)
+            for p in range(len(pieces)):
+                if pieces[p][0] == k:
+                    relay(z, p, 0, has_r)
+                    relay(z, p, 1, has_l)
 
     def hid_part(s):
         total = jnp.zeros((T, E), F32)
@@ -208,15 +221,21 @@
                 preferred_element_type=F32)
         return total
 
-    for d in range(1, N):
+    def hid_send(d):
         s = lax.rem(me_v + d, N)
-        hss[d] = hid_part(s).astype(BF16)
-        send(hss.at[d], hsr.at[d], hs_s.at[d], hs_r.at[d], {"voc": s})
-    own_hs[...] = hid_part(me_v)
-
-    for zz in range(Z):
-        arrived(vgy.at[zz], vy_r.at[zz], vy_s.at[zz])
-        vsum[zz] = vgb[rows_of(zz * 2 + y, R), :].astype(F32) + vgy[zz].astype(F32)
+        if d == 0:
+            own_hs[...] = hid_part(s)
+        else:
+            hss[d] = hid_part(s).astype(BF16)
+            send(hss.at[d], hsr.at[d], hs_s.at[d], hs_r.at[d], {"voc": s})
+
+    hid_order = list(range(1, N)) + [0]
+    hid_per = -(-N // (len(pieces) - 1))
+
+    def pair_sums():
+        for zz in range(Z):
+            arrived(vgy.at[zz], vy_r.at[zz], vy_s.at[zz])
+            vsum[zz] = vgb[rows_of(zz * 2 + y, R), :].astype(F32) + vgy[zz].astype(F32)
 
     def hop(h):
         for way, at, ends in ((0, h, range(h + 1, Z)), (1, Z - 1 - h, range(Z - 1 - h))):
@@ -238,28 +257,33 @@
             for c in copies:
                 sends.append((z == at, c))
 
-    for d in range(1, Z):
-        src = lax.rem(z - d + Z, Z)
-        arrived(hrow.at[:, pl.ds(src * T, T)], hid_r.at[d], hid_s.at[d])
-    for b in range(2):
-        htr[b] = hrow[b].T
-
-    per = pl.cdiv(max(Z - 1, 1), K)
-    for k in range(K):
-        for h in range(k * per, min((k + 1) * per, Z - 1)):
-            hop(h)
+    if Z == 1:
+        for e in hid_order:
+            hid_send(e)
+    per = -(-(Z - 1) // (len(pieces) - 1))
+    for p, (k, lo, wide) in enumerate(pieces):
+        lanes = slice(lo, lo + wide)
         for d in range(1, Z):
             for there, t, way, more in (
                 (z >= d, z - d, 0, has_r), (z + d < Z, z + d, 1, has_l),
             ):
-                def _(t=t, k=k):
-                    arrived(pg.at[k, rows_of(t, T)], ag_r.at[t, k], ag_s.at[0, t, k])
+                def _(t=t):
+                    arrived(pg.at[k, rows_of(t, T), pl.ds(lo, wide)], ag_r.at[t, p], ag_s.at[0, t, p])
                 pl.when(there)(_)
                 if d < Z - 1:
-                    relay(t, k, way, there & more)
-        psend[k] = jnp.dot(htr[1 - y], pg[k], preferred_element_type=F32).astype(BF16)
-        send(psend.at[k], precv.at[k], pp_s.at[k], pp_r.at[k], {"tok": ypart})
-        acc[k] = jnp.dot(htr[y], pg[k], preferred_element_type=F32)
+                    relay(t, p, way, there & more)
+            if d == 1:
+                for e in hid_order[p * hid_per:(p + 1) * hid_per]:
+                    hid_send(e)
+        psend[k, :, lanes] = jnp.dot(
+            htr[1 - y], pg[k, :, lanes], preferred_element_type=F32).astype(BF16)
+        send(psend.at[k, :, pl.ds(lo, wide)], precv.at[k, :, pl.ds(lo, wide)],
+             pp_s.at[p], pp_r.at[p], {"tok": ypart})
+        acc[k, :, lanes] = jnp.dot(htr[y], pg[k, :, lanes], preferred_element_type=F32)
+        if p == 0:
+            pair_sums()
+        for h in range(p * per, min((p + 1) * per, Z - 1)):
+            hop(h)
 
     acc_v = vsum.at[z]
     for way, pred in ((0, has_l), (1, has_r)):
@@ -277,9 +301,10 @@
         htot = htot + column(mgrad[k:k + 1, :], E) * mixf[k:k + 1, :]
     out_hidden[...] = htot.astype(BF16)
 
-    for k in range(K):
-        arrived(precv.at[k], pp_r.at[k], pp_s.at[k])
-        out_proj[k] = (acc[k] + precv[k].astype(F32)).astype(BF16)
+    for p, (k, lo, wide) in enumerate(pieces):
+        lanes = slice(lo, lo + wide)
+        arrived(precv.at[k, :, pl.ds(lo, wide)], pp_r.at[p], pp_s.at[p])
+        out_proj[k, :, lanes] = (acc[k, :, lanes] + precv[k, :, lanes].astype(F32)).astype(BF16)
     for pred, c in sends:
         if pred is None:
             c.wait_send()
@@ -316,7 +341,7 @@
         dma((Z,)), dma((Z,)), dma((N,)), dma((N,)),
         dma((half, K)), dma((half, K)), dma((half, K)), dma((half, K)),
         dma((Z,)), dma((Z,)), dma((2, Z)), dma((2, Z)), dma((N,)), dma((N,)),
-        dma((2, Z, K)), dma((Z, K)), dma((K,)), dma((K,)),
+        dma((2, Z, K + 1)), dma((Z, K + 1)), dma((K + 1,)), dma((K + 1,)),
     ]
     spec = pl.BlockSpec(memory_space=pltpu.VMEM)
     hidden_grad, proj_grad, vocab_grad = pl.pallas_call(

time: 96.5 us -> 92.6 us (0.960)
  Pallas kernels: 84 us -> 80.2 us
    pallas_call x1, Pallas kernels: 84 us -> 80.2 us  [body(): pl.pallas_call(functools.partial(kernel, M, N), out_shape=(jax.ShapeDtype...]
where the time goes in v4:
time: 92.6 us; the launch traced here: 92.4 us
  Pallas kernels  80.2 us (87%)
  local copies, waits for them, and re-layouts  11.5 us (12%)
    pallas_call x1, Pallas kernels, body(): pl.pallas_call(functools.partial(kernel, M, N), out_shape=(jax.ShapeDtype...  80.2 us
    unnamed x16, local copies, waits for them, and re-layouts  11.5 us

profile of v4, /device:TPU:0, one launch (start us, length us, event | category | flops | bytes accessed | tf_op | source)
XLA Modules:
  0.0 92.4 jit_solution(4988675896676467432)
XLA Ops:
  0.6 0.0 copy-start
  0.6 0.0 copy-start.1
  0.7 0.0 copy-start.2
  0.7 0.0 copy-start.3
  0.7 0.0 copy-start.4
  0.7 0.0 copy-start.5
  0.7 8.4 %copy.13 = bf16[2048,4,512]{2,0,1:T(8,128)(2,1)} copy(bf16[2048,4,512]{2,1,0:T(4,128)(2,1)} %param.9) | data formatting | bytes 16777216 | tf_op args[2]
  9.1 0.0 copy-done
  9.1 0.0 copy-done.1
  9.1 0.0 copy-done.2
  9.1 0.0 copy-done.3
  9.1 0.0 copy-done.4
  9.1 0.0 copy-done.5
  9.1 80.2 %shard_map.94 = (bf16[128,512]{1,0:T(8,128)(2,1)S(1)}, bf16[4,256,512]{2,1,0:T(8,128)(2,1)S(1)}, bf16[256,256]{1,0:T(8,128)(2,1)S(1)}) custom-call(bf16[128,2048]{1,0:T(8,128)(2,1)S(1)} %copy-done.1, bf16[4,512]{1,0:T(4,128)(2,1)S(1)} %copy-done.2, bf16[4,2048,512]{2,1,0:T(8,128)(2,1)} %bitcast.9, bf16[2048,256]{1,0:T(8,128)(2,1)S(1)} %copy-done, ...), custom_call_target="tpu_custom_call" | custom-call | tf_op jit(solution)/shard_map/pallas_call | solution.py:347
  89.3 1.8 %copy.11 = bf16[256,4,512]{2,1,0:T(4,128)(2,1)} copy(bf16[256,4,512]{2,0,1:T(8,128)(2,1)S(1)} %bitcast.6) | data formatting | bytes 2097152
  91.1 0.7 copy.16
  91.8 0.7 copy.17
Async XLA Ops:
  0.6 8.5 %copy-start = (bf16[2048,256]{1,0:T(8,128)(2,1)S(1)}, bf16[2048,256]{1,0:T(8,128)(2,1)}, u32[]{:S(2)}) copy-start(bf16[2048,256]{1,0:T(8,128)(2,1)} %vw.1) | copy-start | bytes 3145732
  0.6 8.5 %copy-start.1 = (bf16[128,2048]{1,0:T(8,128)(2,1)S(1)}, bf16[128,2048]{1,0:T(8,128)(2,1)}, u32[]{:S(2)}) copy-start(bf16[128,2048]{1,0:T(8,128)(2,1)} %hidden.1) | copy-start | bytes 1572868
  0.7 8.5 %copy-start.2 = (bf16[4,512]{1,0:T(4,128)(2,1)S(1)}, bf16[4,512]{1,0:T(4,128)(2,1)}, u32[]{:S(2)}) copy-start(bf16[4,512]{1,0:T(4,128)(2,1)} %mix.1) | copy-start | bytes 12292
  0.7 8.5 %copy-start.3 = (f32[4,128]{1,0:T(4,128)S(1)}, f32[4,128]{1,0:T(4,128)}, u32[]{:S(2)}) copy-start(f32[4,128]{1,0:T(4,128)} %logz.1) | copy-start | bytes 6148
  0.7 8.5 %copy-start.4 = (s32[128]{0:T(128)S(1)}, s32[128]{0:T(128)}, u32[]{:S(2)}) copy-start(s32[128]{0:T(128)} %param.12) | copy-start | bytes 1540
  0.7 8.5 %copy-start.5 = (f32[128]{0:T(128)S(1)}, f32[128]{0:T(128)}, u32[]{:S(2)}) copy-start(f32[128]{0:T(128)} %param.13) | copy-start | bytes 1540
